TPU v7x, 32 devices: a whole 2x2x4 slice. The times are simulated.
32 devices in a mesh: dp: 8 (over y, x, core), mp: 4 (over z).
Axes of the slice: x: 2, y: 2, z: 4, core: 2. Of those that a mesh axis runs over, the one named last changes fastest.
Arguments:
- doc_ids: int32 [8, 512], P('dp'), may hold values from 0 to 128255
- doc_lengths: int32 [8], P('dp'), may hold values from 128 to 512
- activations: bfloat16 [4096, 4096], P('dp'), may hold values from -6 to 6
- out_grads: bfloat16 [4096, 14336], P('dp'), may hold values from -0.29882812 to 0.29882812
- input_basis: bfloat16 [4096, 2048], P(None, 'mp'), may hold values from -0.09375 to 0.09375
- output_basis: bfloat16 [14336, 7168], P('dp', 'mp'), may hold values from -0.046875 to 0.046875
- eigenvalues: bfloat16 [2048, 7168], P(None, 'mp'), may hold values from 0.5 to 50
- query_left: bfloat16 [32, 32, 2048], P('dp'), may hold values from -0.125 to 0.125
- query_right: bfloat16 [32, 32, 7168], P('dp', None, 'mp'), may hold values from -0.0625 to 0.0625
Outputs:
- scores: float32 [8, 32], P('dp')
Inputs may be any that keep to these rules, and one draw needn't show every extreme that they name: `doc_lengths`: the live tokens are the first ones of each document.
All inputs are finite; a program needn't handle non-finite values.
Results may differ from a plain program's by a relative error of at most 0.023.
Values may be sent and summed in bfloat16 or wider, within the bound.
A program may use at most 192 MiB of HBM per device.

v0:
```python
import jax
import jax.numpy as jnp
from jax import lax
from jax.sharding import PartitionSpec as P

damping = 0.5


def token_weights(doc_ids, doc_lengths):
    positions = jnp.arange(doc_ids.shape[1], dtype=jnp.int32)
    active = positions[None, :] < doc_lengths[:, None]
    matches = (doc_ids[:, :, None] == doc_ids[:, None, :]) & active[:, None, :]
    repeats = jnp.sum(matches.astype(jnp.float32), axis=2)
    return jnp.where(active, 1.0 / jnp.maximum(repeats, 1.0), 0.0)


def per_device(
    doc_ids,
    doc_lengths,
    activations,
    out_grads,
    input_basis,
    output_basis,
    eigenvalues,
    query_left,
    query_right,
):
    out_cols = output_basis.shape[1]
    rotated_share = jnp.dot(activations, input_basis, preferred_element_type=jnp.float32).astype(
        jnp.bfloat16
    )
    rotated_in = lax.all_gather(rotated_share, "mp", axis=1, tiled=True)
    columns = lax.all_to_all(out_grads, "dp", split_axis=1, concat_axis=0, tiled=True)
    summed = lax.psum_scatter(
        jnp.dot(columns, output_basis, preferred_element_type=jnp.float32).astype(jnp.bfloat16),
        "dp",
        scatter_dimension=0,
        tiled=True,
    )
    weights = token_weights(doc_ids, doc_lengths)
    docs_here = doc_ids.shape[0]
    acts_doc = rotated_in.reshape(docs_here, -1, rotated_in.shape[1])
    grads_doc = summed.reshape(docs_here, -1, out_cols)
    scaled = (weights[:, :, None] * grads_doc.astype(jnp.float32)).astype(jnp.bfloat16)
    gradient = jnp.einsum("dti,dtj->dij", acts_doc, scaled, preferred_element_type=jnp.float32)
    conditioned = (gradient / (eigenvalues.astype(jnp.float32) + damping)).astype(jnp.bfloat16)
    rank_rows = query_left.shape[1]
    left_part = lax.all_gather(query_left, "dp", axis=0, tiled=True)
    right_part = lax.all_gather(query_right, "dp", axis=0, tiled=True)
    number = left_part.shape[0]
    left_rows = left_part.reshape(number * rank_rows, left_part.shape[2])
    right_rows = right_part.reshape(number * rank_rows, right_part.shape[2]).astype(jnp.float32)
    mixture = jnp.einsum("ri,dij->drj", left_rows, conditioned, preferred_element_type=jnp.float32)
    values = jnp.sum((mixture * right_rows[None]).reshape(docs_here, number, -1), axis=2)
    return lax.psum(values, "mp")


def solution(mesh):
    return jax.shard_map(
        per_device,
        mesh=mesh,
        in_specs=(
            P("dp", None),
            P("dp"),
            P("dp", None),
            P("dp", None),
            P(None, "mp"),
            P("dp", "mp"),
            P(None, "mp"),
            P("dp", None, None),
            P("dp", None, "mp"),
        ),
        out_specs=P("dp", None),
        check_vma=False,
    )
```

profile of v0, /device:TPU:0, one launch (start us, length us, event | category | flops | bytes accessed | tf_op | source)
XLA Modules:
  0.0 409.6 jit_solution(17460435752555275028)
XLA Ops:
  6.5 20.0 %copy.18 = bf16[512,14336]{0,1:T(8,128)(2,1)} copy(bf16[512,14336]{1,0:T(8,128)(2,1)} %param.12) | data formatting | bytes 29360128 | tf_op args[3]
  26.5 5.6 %all-to-all-start = ((bf16[512,8,1792]{0,2,1:T(8,128)(2,1)}), bf16[512,8,1792]{0,2,1:T(8,128)(2,1)}, u32[]{:S(2)}, u32[]{:S(2)}) async-start(bf16[512,8,1792]{0,2,1:T(8,128)(2,1)} %bitcast.25), calls=%async_computation | async-start | bytes 29360128 | tf_op jit(solution)/shard_map/all_to_all | solution.py:33
  32.1 0.0 all-gather.8.cloned.1.call-start
  32.1 0.7 all-gather.8.cloned.1.call-update
  32.8 0.0 all-gather.4.cloned.1.call-start
  32.8 6.6 %convolution_convert_fusion.1 = bf16[512,512]{1,0:T(8,128)(2,1)} fusion(bf16[512,4096]{1,0:T(8,128)(2,1)} %param.11, bf16[4096,512]{1,0:T(8,128)(2,1)} %param.13), kind=kOutput, calls=%fused_computation.9 | convolution fusion | flops 2147745792 | bytes 8912896 | tf_op jit(solution)/shard_map/dot_general | solution.py:29
  39.4 0.0 all-gather.4.cloned.1.call-update
  39.5 0.0 all-gather.6.cloned.1.call-start
  39.5 0.7 all-gather.6.cloned.1.call-update
  40.2 0.0 reduce-scatter.2.cloned.1.call-start
  40.3 174.3 %all-to-all-done = bf16[512,8,1792]{0,2,1:T(8,128)(2,1)} async-done(((bf16[512,8,1792]{0,2,1:T(8,128)(2,1)}), bf16[512,8,1792]{0,2,1:T(8,128)(2,1)}, u32[]{:S(2)}, u32[]{:S(2)}) %all-to-all-start) | async-done | bytes 14680096 | tf_op jit(solution)/shard_map/all_to_all | solution.py:33
  214.6 18.9 %copy.19 = bf16[8,512,1792]{2,1,0:T(8,128)(2,1)} copy(bf16[8,512,1792]{1,2,0:T(8,128)(2,1)} %bitcast.3) | data formatting | bytes 29360128 | tf_op jit(solution)/shard_map/all_to_all | solution.py:33
  233.4 33.0 %convolution_convert_fusion = bf16[4096,1792]{1,0:T(8,128)(2,1)} fusion(bf16[4096,1792]{1,0:T(8,128)(2,1)} %bitcast.26, bf16[1792,1792]{1,0:T(8,128)(2,1)} %param.14), kind=kOutput, calls=%fused_computation | convolution fusion | flops 26314014720 | bytes 35782656 | tf_op jit(solution)/shard_map/dot_general | solution.py:35
  266.5 0.0 copy-start
  266.5 0.0 reduce-scatter.2.cloned.1.call-update
  267.1 0.0 copy-done
  267.2 0.3 convert_reduce_fusion
  267.5 0.0 all-gather.8.cloned.1.call-done
  267.5 6.2 %bitcast_convert_fusion = f32[1,1024,1792]{2,1,0:T(8,128)} fusion(bf16[1,1024,1792]{2,1,0:T(8,128)(2,1)} %bitcast.27), kind=kLoop, calls=%fused_computation.6 | loop fusion | flops 1835008 | bytes 11010048 | tf_op jit(solution)/shard_map/convert_element_type | solution.py:52
  273.7 9.0 %copy.20 = f32[1,1024,1792]{1,2,0:T(8,128)} copy(f32[1,1024,1792]{2,1,0:T(8,128)} %bitcast_convert_fusion) | data formatting | bytes 14680064 | tf_op jit(solution)/shard_map/convert_element_type | solution.py:52
  282.7 0.0 all-gather.4.cloned.1.call-done
  282.7 0.0 all-gather.6.cloned.1.call-done
  282.7 88.7 %reduce-scatter.2.cloned.1.call-done = bf16[512,1792]{1,0:T(8,128)(2,1)} async-done(((bf16[4096,1792]{1,0:T(8,128)(2,1)}), bf16[512,1792]{1,0:T(8,128)(2,1)}) %reduce-scatter.2.cloned.1.call-update) | async-done | bytes 1835024 | tf_op jit(solution)/shard_map/reduce_scatter | solution.py:34
  371.5 19.2 %fusion = f32[1024]{0:T(1024)S(1)} fusion(f32[1,1024,1792]{1,2,0:T(8,128)} %copy.20, bf16[1024,2048]{1,0:T(8,128)(2,1)} %bitcast.30, bf16[2048,1792]{1,0:T(8,128)(2,1)} %param.15, bf16[512,2048]{1,0:T(8,128)(2,1)} %all-gather.4.cloned.1.call-done, bf16[512,1792]{1,0:T(8,128)(2,1)} %reduce-scatter.2.cloned.1.call-done, f32[512]{0:T(512)S(1)} %divide_select_fusion), kind=kOutput, calls=%fused_computation.3 | convolution fusion | flops 11295390720 | bytes 22812672 | tf_op jit(solution)/shard_map/ri,dij->drj/dot_general | solution.py:53
  390.7 0.1 reduce_sum.29
  390.7 0.1 reduce_sum.30
  390.9 12.2 %psum.7 = f32[1,32]{1,0:T(1,128)} all-reduce(f32[1,32]{1,0:T(1,128)S(1)} %bitcast.29), channel_id=1, replica_groups=mesh['dp'=8,'mp'=4] {'mp'}, use_global_device_ids=true, to_apply=%region_4.5 | all-reduce | flops 32 | bytes 256 | tf_op jit(solution)/shard_map/psum | solution.py:55
  (2 shorter events, 0.0 us)
Async XLA Ops:
  26.5 188.1 %all-to-all-start = ((bf16[512,8,1792]{0,2,1:T(8,128)(2,1)}), bf16[512,8,1792]{0,2,1:T(8,128)(2,1)}, u32[]{:S(2)}, u32[]{:S(2)}) async-start(bf16[512,8,1792]{0,2,1:T(8,128)(2,1)} %bitcast.25), calls=%async_computation | async-start | bytes 29360128 | tf_op jit(solution)/shard_map/all_to_all | solution.py:33
  32.1 235.4 %all-gather.8.cloned.1.call-start = ((), (), s32[]{:S(2)}) async-start(), calls=%async_computation.5 | async-start | bytes 4128768 | tf_op jit(solution)/shard_map/all_gather | solution.py:49
  32.8 249.9 %all-gather.4.cloned.1.call-start = ((), (), s32[]{:S(2)}) async-start(), calls=%async_computation.2 | async-start | bytes 2621440 | tf_op jit(solution)/shard_map/all_gather | solution.py:32
  39.5 243.3 %all-gather.6.cloned.1.call-start = ((), (), s32[]{:S(2)}) async-start(), calls=%async_computation.4 | async-start | bytes 4718592 | tf_op jit(solution)/shard_map/all_gather | solution.py:48
  40.2 331.2 %reduce-scatter.2.cloned.1.call-start = ((), (), s32[]{:S(2)}) async-start(), calls=%async_computation.3 | async-start | bytes 16515072 | tf_op jit(solution)/shard_map/reduce_scatter | solution.py:34
  266.5 0.7 copy-start
Sparse Core Ops, SparseCore 0:
  34.7 106.9 all-gather.7
  143.3 45.7 all-gather.3
  191.0 41.0 all-gather.5
  266.6 104.8 reduce-scatter.1
where the time goes:
time: 411 us; the launch traced here: 410 us
  waiting for transfers between devices  264 us (64%)
  matrix products  58.8 us (14%)
  local copies, waits for them, and re-layouts  47.9 us (12%)
  between operations  13.8 us (3%)
  blocking collectives  12.2 us (3%)
  other arithmetic  6.67 us (2%)
  starting transfers between devices  5.72 us (1%)
    all_to_all x1, waiting for transfers between devices, per_device(): lax.all_to_all(out_grads, 'dp', split_axis=1, concat_axis=0, tiled=True)  174 us
    reduce_scatter x1, waiting for transfers between devices, per_device(): lax.psum_scatter(jnp.dot(columns, output_basis, preferred_element_type=jn...  88.7 us
    dot_general x1, matrix products, per_device(): jnp.dot(columns, output_basis, preferred_element_type=jnp.float32)  33 us
    unnamed x3, local copies, waits for them, and re-layouts  20 us
    dot_general x1, matrix products, per_device(): jnp.einsum('ri,dij->drj', left_rows, conditioned, preferred_element_type=...  19.2 us
    all_to_all x1, local copies, waits for them, and re-layouts, per_device(): lax.all_to_all(out_grads, 'dp', split_axis=1, concat_axis=0, tiled=True)  18.9 us
    psum x1, blocking collectives, per_device(): return lax.psum(values, 'mp')  12.2 us
    convert_element_type x1, local copies, waits for them, and re-layouts, per_device(): right_part.reshape(number * rank_rows, right_part.shape[2])  8.99 us
  transfers between devices with their start and end apart: 5, of which 2 were waited for; matrix products, arithmetic and copies ran while one was open for 18% of the time, Pallas kernels for 0%

commit v1 on v0

--- a/solution.py
+++ b/solution.py
@@ -30,7 +30,10 @@
         jnp.bfloat16
     )
     rotated_in = lax.all_gather(rotated_share, "mp", axis=1, tiled=True)
-    columns = lax.all_to_all(out_grads, "dp", split_axis=1, concat_axis=0, tiled=True)
+    peers = lax.axis_size("dp")
+    parts = jnp.stack(jnp.split(out_grads, peers, axis=1), axis=0)
+    parts = lax.all_to_all(parts, "dp", split_axis=0, concat_axis=0)
+    columns = jnp.concatenate(parts, axis=0)
     summed = lax.psum_scatter(
         jnp.dot(columns, output_basis, preferred_element_type=jnp.float32).astype(jnp.bfloat16),
         "dp",

time: 411 us -> 395 us (0.961)
  local copies, waits for them, and re-layouts: 47.9 us -> 32.2 us
    all_to_all x1 -> x0, local copies, waits for them, and re-layouts: 18.9 us -> none  [per_device(): lax.all_to_all(out_grads, 'dp', split_axis=1, concat_axis=0, tiled=True)]
    unnamed x3 -> x9, local copies, waits for them, and re-layouts: 20 us -> 20.2 us
  transfers between devices with their start and end apart: 5 -> 5, of which waited for: 2 -> 2; matrix products, arithmetic and copies ran while one was open for 18% -> 14% of each run, Pallas kernels for 0% -> 0%
where the time goes in v1:
time: 395 us; the launch traced here: 394 us
  waiting for transfers between devices  264 us (67%)
  matrix products  59.5 us (15%)
  local copies, waits for them, and re-layouts  32.2 us (8%)
  between operations  13.8 us (3%)
  blocking collectives  12.2 us (3%)
  other arithmetic  6.67 us (2%)
  starting transfers between devices  5.87 us (1%)
    all_to_all x1, waiting for transfers between devices, per_device(): parts = lax.all_to_all(parts, 'dp', split_axis=0, concat_axis=0)  174 us
    reduce_scatter x1, waiting for transfers between devices, per_device(): lax.psum_scatter(jnp.dot(columns, output_basis, preferred_element_type=jn...  88.6 us
    dot_general x1, matrix products, per_device(): jnp.dot(columns, output_basis, preferred_element_type=jnp.float32)  33.7 us
    unnamed x9, local copies, waits for them, and re-layouts  20.2 us
    dot_general x1, matrix products, per_device(): jnp.einsum('ri,dij->drj', left_rows, conditioned, preferred_element_type=...  19.2 us
    psum x1, blocking collectives, per_device(): return lax.psum(values, 'mp')  12.2 us
    convert_element_type x1, local copies, waits for them, and re-layouts, per_device(): right_part.reshape(number * rank_rows, right_part.shape[2])  9.09 us
  transfers between devices with their start and end apart: 5, of which 2 were waited for; matrix products, arithmetic and copies ran while one was open for 14% of the time, Pallas kernels for 0%

profile of v1, /device:TPU:0, one launch (start us, length us, event | category | flops | bytes accessed | tf_op | source)
XLA Modules:
  0.0 394.4 jit_solution(15562632746858937557)
XLA Ops:
  6.5 2.9 bitcast_dynamic-update-slice_fusion.7
  9.4 2.8 bitcast_dynamic-update-slice_fusion.6
  12.3 2.9 bitcast_dynamic-update-slice_fusion.5
  15.1 2.9 bitcast_dynamic-update-slice_fusion.4
  18.0 2.9 bitcast_dynamic-update-slice_fusion.3
  21.0 2.9 bitcast_dynamic-update-slice_fusion.2
  23.8 2.9 bitcast_dynamic-update-slice_fusion.1
  26.7 2.9 bitcast_dynamic-update-slice_fusion
  29.6 5.5 %all-to-all-start = ((bf16[8,512,1792]{2,1,0:T(8,128)(2,1)}), bf16[8,512,1792]{2,1,0:T(8,128)(2,1)}, u32[]{:S(2)}, u32[]{:S(2)}) async-start(bf16[8,512,1792]{2,1,0:T(8,128)(2,1)} %bitcast_dynamic-update-slice_fusion), calls=%async_computation | async-start | bytes 29360128 | tf_op jit(solution)/shard_map/all_to_all | solution.py:35
  35.1 0.0 all-gather.8.cloned.1.call-start
  35.2 0.7 all-gather.8.cloned.1.call-update
  35.9 0.0 all-gather.4.cloned.1.call-start
  35.9 6.6 %convolution_convert_fusion.1 = bf16[512,512]{1,0:T(8,128)(2,1)} fusion(bf16[512,4096]{1,0:T(8,128)(2,1)} %param.11, bf16[4096,512]{1,0:T(8,128)(2,1)} %param.13), kind=kOutput, calls=%fused_computation.17 | convolution fusion | flops 2147745792 | bytes 8912896 | tf_op jit(solution)/shard_map/dot_general | solution.py:29
  42.5 0.0 all-gather.4.cloned.1.call-update
  42.5 0.0 all-gather.6.cloned.1.call-start
  42.6 0.7 all-gather.6.cloned.1.call-update
  43.3 0.2 reduce-scatter.2.cloned.1.call-start
  43.5 174.1 %all-to-all-done = bf16[8,512,1792]{2,1,0:T(8,128)(2,1)} async-done(((bf16[8,512,1792]{2,1,0:T(8,128)(2,1)}), bf16[8,512,1792]{2,1,0:T(8,128)(2,1)}, u32[]{:S(2)}, u32[]{:S(2)}) %all-to-all-start) | async-done | bytes 14680096 | tf_op jit(solution)/shard_map/all_to_all | solution.py:35
  217.6 33.7 %convolution_convert_fusion = bf16[4096,1792]{1,0:T(8,128)(2,1)} fusion(bf16[4096,1792]{1,0:T(8,128)(2,1)} %bitcast.10, bf16[1792,1792]{1,0:T(8,128)(2,1)} %param.14), kind=kOutput, calls=%fused_computation | convolution fusion | flops 26314014720 | bytes 35782656 | tf_op jit(solution)/shard_map/dot_general | solution.py:38
  251.3 0.0 copy-start
  251.3 0.0 reduce-scatter.2.cloned.1.call-update
  252.0 0.0 copy-done
  252.0 0.3 convert_reduce_fusion
  252.4 0.0 all-gather.8.cloned.1.call-done
  252.4 6.2 %bitcast_convert_fusion = f32[1,1024,1792]{2,1,0:T(8,128)} fusion(bf16[1,1024,1792]{2,1,0:T(8,128)(2,1)} %bitcast.39), kind=kLoop, calls=%fused_computation.6 | loop fusion | flops 1835008 | bytes 11010048 | tf_op jit(solution)/shard_map/convert_element_type | solution.py:55
  258.6 9.1 %copy.13 = f32[1,1024,1792]{1,2,0:T(8,128)} copy(f32[1,1024,1792]{2,1,0:T(8,128)} %bitcast_convert_fusion) | data formatting | bytes 14680064 | tf_op jit(solution)/shard_map/convert_element_type | solution.py:55
  267.7 0.0 all-gather.4.cloned.1.call-done
  267.7 0.0 all-gather.6.cloned.1.call-done
  267.7 88.6 %reduce-scatter.2.cloned.1.call-done = bf16[512,1792]{1,0:T(8,128)(2,1)} async-done(((bf16[4096,1792]{1,0:T(8,128)(2,1)}), bf16[512,1792]{1,0:T(8,128)(2,1)}) %reduce-scatter.2.cloned.1.call-update) | async-done | bytes 1835024 | tf_op jit(solution)/shard_map/reduce_scatter | solution.py:37
  356.3 19.2 %fusion = f32[1024]{0:T(1024)S(1)} fusion(f32[1,1024,1792]{1,2,0:T(8,128)} %copy.13, bf16[1024,2048]{1,0:T(8,128)(2,1)} %bitcast.42, bf16[2048,1792]{1,0:T(8,128)(2,1)} %param.15, bf16[512,2048]{1,0:T(8,128)(2,1)} %all-gather.4.cloned.1.call-done, bf16[512,1792]{1,0:T(8,128)(2,1)} %reduce-scatter.2.cloned.1.call-done, f32[512]{0:T(512)S(1)} %divide_select_fusion), kind=kOutput, calls=%fused_computation.3 | convolution fusion | flops 11295390720 | bytes 22812672 | tf_op jit(solution)/shard_map/ri,dij->drj/dot_general | solution.py:56
  375.5 0.1 reduce_sum.29
  375.6 0.1 reduce_sum.30
  375.7 12.2 %psum.7 = f32[1,32]{1,0:T(1,128)} all-reduce(f32[1,32]{1,0:T(1,128)S(1)} %bitcast.41), channel_id=1, replica_groups=mesh['dp'=8,'mp'=4] {'mp'}, use_global_device_ids=true, to_apply=%region_4.5 | all-reduce | flops 32 | bytes 256 | tf_op jit(solution)/shard_map/psum | solution.py:58
  (2 shorter events, 0.0 us)
Async XLA Ops:
  29.6 188.1 %all-to-all-start = ((bf16[8,512,1792]{2,1,0:T(8,128)(2,1)}), bf16[8,512,1792]{2,1,0:T(8,128)(2,1)}, u32[]{:S(2)}, u32[]{:S(2)}) async-start(bf16[8,512,1792]{2,1,0:T(8,128)(2,1)} %bitcast_dynamic-update-slice_fusion), calls=%async_computation | async-start | bytes 29360128 | tf_op jit(solution)/shard_map/all_to_all | solution.py:35
  35.1 217.3 %all-gather.8.cloned.1.call-start = ((), (), s32[]{:S(2)}) async-start(), calls=%async_computation.5 | async-start | bytes 4128768 | tf_op jit(solution)/shard_map/all_gather | solution.py:52
  35.9 231.9 %all-gather.4.cloned.1.call-start = ((), (), s32[]{:S(2)}) async-start(), calls=%async_computation.2 | async-start | bytes 2621440 | tf_op jit(solution)/shard_map/all_gather | solution.py:32
  42.5 225.2 %all-gather.6.cloned.1.call-start = ((), (), s32[]{:S(2)}) async-start(), calls=%async_computation.4 | async-start | bytes 4718592 | tf_op jit(solution)/shard_map/all_gather | solution.py:51
  43.3 313.0 %reduce-scatter.2.cloned.1.call-start = ((), (), s32[]{:S(2)}) async-start(), calls=%async_computation.3 | async-start | bytes 16515072 | tf_op jit(solution)/shard_map/reduce_scatter | solution.py:37
  251.3 0.7 copy-start
Sparse Core Ops, SparseCore 0:
  37.8 106.9 all-gather.7
  146.4 45.7 all-gather.3
  194.1 41.0 all-gather.5
  251.5 104.7 reduce-scatter.1
